TPU v7x, 512 devices: a 4x2x32 block of a 4x8x32 slice. The times are simulated.
512 devices in a mesh: grp: 2 (over y), sp: 128 (over x, z), ch: 2 (over core).
Axes of the slice: x: 4, y: 2, z: 32, core: 2. Of those that a mesh axis runs over, the one named last changes fastest.
The devices are a block of a 4x8x32 slice.
Arguments:
- latents: bfloat16 [262144, 1024], P(('grp', 'sp')), parts along dimension 0, may hold values from -6 to 6
- spectrum: bfloat16 [16, 64, 128, 1024], P(None, None, 'sp', 'ch'), may hold values from -4 to 4
- w_value: bfloat16 [1024, 1024], P('sp', 'ch'), may hold values from -0.1875 to 0.1875
- w_gate: bfloat16 [1024, 1024], P('sp', 'ch'), may hold values from -0.1875 to 0.1875
- w_out: bfloat16 [1024, 1024], P('sp'), may hold values from -0.1875 to 0.1875
- embed_table: bfloat16 [1024, 32768], P(('sp', 'ch')), may hold values from -12 to 12
- prompt_ids: int32 [512], P('grp'), parts along dimension 0, may hold values from 0 to 32767
- noise_step: int32 [2], P('grp'), parts along dimension 0, may hold values from 0 to 999
Outputs:
- denoised: bfloat16 [262144, 1024], P(('grp', 'sp', 'ch')), parts along dimension 0
There are 2 independent parts, one for each index of `grp`. A program takes and returns all parts, laid end to end along the dimension named above; an argument that names none is the same for every part. Nothing has to cross between parts.
All inputs are finite; a program needn't handle non-finite values.
Results may differ from a plain program's by a relative error of at most 0.013.
Values may be sent and summed in bfloat16 or wider, within the bound.
A program may use at most 64 MiB of HBM per device.

v0:
```python
import math
import jax
import jax.numpy as jnp
from jax import lax
from jax.sharding import Mesh
from jax.sharding import PartitionSpec as P

TT = 16
HH = 64
WW = 128
C = 1024
SP = ("sp_0", "sp_1")
SP_CH = ("sp_0", "sp_1", "ch")
GRP_SP = ("grp", "sp_0", "sp_1")
GRP_SP_CH = ("grp", "sp_0", "sp_1", "ch")


def in_one_piece(arrays, axis, dim, along):
    ends, at = ([], 0)
    for a in arrays[:-1]:
        at += a.shape[along]
        ends.append(at)
    both = jnp.concatenate(arrays, axis=along)
    return tuple(jnp.split(lax.all_gather(both, axis, axis=dim, tiled=True), ends, axis=along))


def joined_along(parts, dim):
    lengths = list(parts.shape[1:])
    lengths[dim] *= parts.shape[0]
    return jnp.moveaxis(parts, 0, dim).reshape(lengths)


def gather_in_order(value, axes, sequence):
    parts = value[None]
    for k in sequence:
        parts = lax.all_gather(parts, axes[k], axis=0, tiled=True)
    held = [lax.axis_size(axes[k]) for k in reversed(sequence)]
    parts = parts.reshape(*held, *value.shape)
    turned = sorted(range(len(sequence)), key=lambda place: sequence[len(sequence) - 1 - place])
    return parts.transpose(*turned, *range(len(sequence), parts.ndim)).reshape(-1, *value.shape)


def gather_axes(value, axes, sequence, dim):
    return joined_along(gather_in_order(value, axes, sequence), dim)


def cas_table(length):
    position = jnp.arange(length, dtype=jnp.int32)
    product = position[:, None] * position[None, :] % length
    phase_angle = product.astype(jnp.float32) * (2.0 * math.pi / length)
    return ((jnp.cos(phase_angle) + jnp.sin(phase_angle)) / math.sqrt(length)).astype(jnp.bfloat16)


def step_embedding(noise_step, channel, channels):
    half_count = channels // 2
    lower_half = channel < half_count
    position = jnp.where(lower_half, channel, channel - half_count).astype(jnp.float32)
    frequency = jnp.exp(-math.log(10000.0) * position / half_count)
    phase_angle = noise_step[0].astype(jnp.float32) * frequency
    return jnp.where(lower_half, jnp.sin(phase_angle), jnp.cos(phase_angle))


def apply_table(form, table, operand):
    return jnp.einsum(form, table, operand, preferred_element_type=jnp.float32)


def local(latents, spectrum, w_value, w_gate, w_out, embed_table, prompt_ids, noise_step):
    row_count = latents.shape[0]
    chan_part = w_value.shape[1]
    full_value, full_gate, full_out = in_one_piece((w_value, w_gate, w_out), SP, 0, 1)
    value_rows = jnp.dot(latents, full_value, preferred_element_type=jnp.float32).astype(
        jnp.bfloat16
    )
    gate_rows = jnp.dot(latents, full_gate, preferred_element_type=jnp.float32)
    cas_width = cas_table(WW)
    cas_height = cas_table(HH)
    cas_time = cas_table(TT)
    line_grid = value_rows.reshape(row_count // WW, WW, chan_part)
    width_spec = apply_table("kw,lwc->lkc", cas_width, line_grid).astype(jnp.bfloat16)
    pencil = lax.all_to_all(width_spec, SP, split_axis=1, concat_axis=0, tiled=True)
    band_count = pencil.shape[1]
    pencil = pencil.reshape(TT, HH, band_count, chan_part)
    height_spec = apply_table("ah,thkc->takc", cas_height, pencil).astype(jnp.bfloat16)
    full_spec = apply_table("st,takc->sakc", cas_time, height_spec).astype(jnp.bfloat16)
    filtered = (full_spec.astype(jnp.float32) * spectrum.astype(jnp.float32)).astype(jnp.bfloat16)
    time_back = apply_table("ts,sakc->takc", cas_time, filtered).astype(jnp.bfloat16)
    height_back = apply_table("ha,takc->thkc", cas_height, time_back).astype(jnp.bfloat16)
    returned = lax.all_to_all(
        height_back.reshape(TT * HH, band_count, chan_part),
        SP,
        split_axis=0,
        concat_axis=1,
        tiled=True,
    )
    mix_rows = apply_table("wk,lkc->lwc", cas_width, returned).reshape(row_count, chan_part)
    offset = lax.axis_index("ch") * chan_part
    local_pool = jnp.mean(jnp.take(embed_table, prompt_ids, axis=1).astype(jnp.float32), axis=1)
    pooled_all = gather_axes(local_pool, SP_CH, (0, 1, 2), 0)
    pooled = lax.dynamic_slice_in_dim(pooled_all, offset, chan_part)
    channel = offset + jnp.arange(chan_part, dtype=jnp.int32)
    modulation = 1.0 + pooled + step_embedding(noise_step, channel, C)
    mixed_rows = (mix_rows * jax.nn.silu(gate_rows) * modulation[None, :]).astype(jnp.bfloat16)
    half_rows = row_count // lax.axis_size("ch")
    moved_rows = lax.all_to_all(mixed_rows, "ch", split_axis=0, concat_axis=1, tiled=True)
    summed = jnp.dot(moved_rows, full_out, preferred_element_type=jnp.float32)
    residual = lax.dynamic_slice_in_dim(latents, lax.axis_index("ch") * half_rows, half_rows, 0)
    return (residual.astype(jnp.float32) + summed).astype(jnp.bfloat16)


def solution(mesh):
    torus = Mesh(
        mesh.devices.reshape(mesh.shape["grp"], 4, 32, mesh.shape["ch"]),
        ("grp", "sp_0", "sp_1", "ch"),
    )
    in_specs = (
        P(GRP_SP, None),
        P(None, None, SP, "ch"),
        P(SP, "ch"),
        P(SP, "ch"),
        P(SP, None),
        P(SP_CH, None),
        P("grp"),
        P("grp"),
    )
    out_specs = P(GRP_SP_CH, None)
    return jax.shard_map(local, mesh=torus, in_specs=in_specs, out_specs=out_specs, check_vma=False)
```

profile of v0, /device:TPU:39, one launch (start us, length us, event | category | flops | bytes accessed | tf_op | source)
XLA Modules:
  0.0 582.0 jit_solution(15386378072836665653)
XLA Ops:
  6.5 0.0 all-gather.4.cloned.1.call-start
  6.6 1.3 pad_maximum_fusion
  7.9 0.1 all-gather.4.cloned.1.call-update
  8.0 275.0 %all-gather.4.cloned.1.call-done = bf16[1024,2048]{1,0:T(8,128)(2,1)} async-done(((bf16[8,2048]{1,0:T(8,128)(2,1)}), bf16[1024,2048]{1,0:T(8,128)(2,1)}) %all-gather.4.cloned.1.call-update) | async-done | bytes 4194320 | tf_op jit(solution)/shard_map/all_gather | solution.py:24
  282.9 3.2 fusion.11
  286.2 0.7 fusion.12
  286.9 0.9 copy.34
  287.8 0.0 copy-start
  287.8 104.4 %all_to_all.52 = bf16[8,128,512]{2,0,1:T(8,128)(2,1)S(1)} all-to-all(bf16[8,128,512]{2,0,1:T(8,128)(2,1)S(1)} %copy.34), channel_id=1, replica_groups=mesh['grp'=2,'sp_0'=4,'sp_1'=32,'ch'=2] {'sp_0','sp_1'}, dimensions={1} | all-to-all | bytes 2097152 | tf_op jit(solution)/shard_map/all_to_all | solution.py:80
  392.2 0.5 fusion.14
  392.8 0.0 copy-done
  392.8 1.6 convolution_convert_fusion.2
  394.4 1.5 convolution_convert_fusion
  395.9 0.5 broadcast.90
  396.4 1.5 reduce.1
  397.9 0.0 copy-start.1
  397.9 1.2 reshape.84
  399.1 16.2 %all-to-all-start.1 = ((bf16[128,2,2048]{2,1,0:T(2,128)(2,1)}), bf16[128,2,2048]{2,1,0:T(2,128)(2,1)S(1)}, u32[]{:S(2)}, u32[]{:S(2)}) async-start(bf16[128,2,2048]{2,1,0:T(2,128)(2,1)} %reshape.84), calls=%async_computation.1 | async-start | bytes 2097152 | tf_op jit(solution)/shard_map/all_to_all | solution.py:88
  415.3 0.0 copy-done.1
  415.3 0.0 copy-start.2
  415.3 5.7 copy.41
  421.1 1.3 dynamic-slice
  423.0 0.0 copy-done.2
  423.1 5.2 gather_fusion
  428.3 0.1 convert_reduce_fusion
  428.4 0.1 multiply_dynamic-update-slice_fusion
  428.5 6.2 %all-reduce = f32[16]{0:T(128)S(1)} all-reduce(f32[16]{0:T(128)S(1)} %multiply_dynamic-update-slice_fusion), channel_id=2, replica_groups=mesh['grp'=2,'sp_0'=4,'sp_1'=32,'ch'=2] {'sp_0'}, use_global_device_ids=true, to_apply=%add | all-reduce | flops 16 | bytes 128
  434.7 0.1 reshape.76
  434.8 97.6 %all-gather.1 = f32[32,4,4]{2,1,0:T(4,128)S(1)} all-gather(f32[1,4,4]{2,1,0:T(4,128)S(1)} %reshape.76), channel_id=1, replica_groups=mesh['grp'=2,'sp_0'=4,'sp_1'=32,'ch'=2] {'sp_1'}, dimensions={0}, use_global_device_ids=true | all-gather | bytes 2112 | tf_op jit(solution)/shard_map/all_gather | solution.py:36
  532.4 0.1 copy.42
  532.5 25.2 %all_gather.15 = f32[256,4]{0,1:T(4,128)S(1)} all-gather(f32[128,4]{0,1:T(4,128)S(1)} %copy.42), channel_id=1, replica_groups=mesh['grp'=2,'sp_0'=4,'sp_1'=32,'ch'=2] {'ch'}, dimensions={0}, use_global_device_ids=true | all-gather | bytes 6144 | tf_op jit(solution)/shard_map/all_gather | solution.py:36
  557.7 0.1 reshape.61
  557.8 0.6 copy.43
  558.4 0.2 reshape_reshape.3
  559.3 0.1 fusion.76
  559.3 0.0 all-to-all-done.1
  559.4 1.1 reshape.85
  560.4 0.3 copy.68
  560.7 1.1 fusion.20
  561.8 1.9 copy.40
  563.7 0.0 copy-start.4
  563.7 4.3 fusion.8
  568.0 0.0 copy-start.3
  568.0 0.1 copy.67
  568.1 4.8 all_to_all.53
  572.9 0.0 copy-done.4
  572.9 0.0 copy-done.3
  572.9 2.2 add_convert_fusion
  (4 shorter events, 0.0 us)
Async XLA Ops:
  6.5 276.4 %all-gather.4.cloned.1.call-start = ((), (), s32[]{:S(2)}) async-start(), calls=%async_computation.3 | async-start | bytes 4227072 | tf_op jit(solution)/shard_map/all_gather | solution.py:24
  287.8 105.0 %copy-start = (bf16[16,64,1,512]{3,1,2,0:T(8,128)(2,1)S(1)}, bf16[16,64,1,512]{3,1,2,0:T(8,128)(2,1)}, u32[]{:S(2)}) copy-start(bf16[16,64,1,512]{3,1,2,0:T(8,128)(2,1)} %param.9) | copy-start | bytes 3145732
  397.9 17.5 %copy-start.1 = (bf16[4,32768]{1,0:T(4,128)(2,1)S(1)}, bf16[4,32768]{1,0:T(4,128)(2,1)}, u32[]{:S(2)}) copy-start(bf16[4,32768]{1,0:T(4,128)(2,1)} %param.13) | copy-start | bytes 786436
  399.1 160.3 %all-to-all-start.1 = ((bf16[128,2,2048]{2,1,0:T(2,128)(2,1)}), bf16[128,2,2048]{2,1,0:T(2,128)(2,1)S(1)}, u32[]{:S(2)}, u32[]{:S(2)}) async-start(bf16[128,2,2048]{2,1,0:T(2,128)(2,1)} %reshape.84), calls=%async_computation.1 | async-start | bytes 2097152 | tf_op jit(solution)/shard_map/all_to_all | solution.py:88
  415.3 7.7 %copy-start.2 = (s32[256]{0:T(256)S(1)}, s32[256]{0:T(256)}, u32[]{:S(2)}) copy-start(s32[256]{0:T(256)} %param.14) | copy-start | bytes 3076
  563.7 9.3 %copy-start.4 = (bf16[1024,1024]{1,0:T(8,128)(2,1)S(1)}, bf16[1024,1024]{1,0:T(8,128)(2,1)}, u32[]{:S(2)}) copy-start(bf16[1024,1024]{1,0:T(8,128)(2,1)} %param.8) | copy-start | bytes 6291460
  568.0 4.9 copy-start.3
Sparse Core Ops, SparseCore 0:
  10.3 272.5 all-gather.3
where the time goes:
time: 583 us; the launch traced here: 582 us
  waiting for transfers between devices  275 us (47%)
  blocking collectives  238 us (41%)
  local copies, waits for them, and re-layouts  19.3 us (3%)
  starting transfers between devices  16.2 us (3%)
  matrix products  15.2 us (3%)
  between operations  14.9 us (3%)
    all_gather x1, waiting for transfers between devices, in_one_piece(): lax.all_gather(both, axis, axis=dim, tiled=True)  275 us
    all_gather x2, blocking collectives, gather_in_order(): parts = lax.all_gather(parts, axes[k], axis=0, tiled=True)  123 us
    all_to_all x1, blocking collectives, local(): lax.all_to_all(width_spec, SP, split_axis=1, concat_axis=0, tiled=True)  104 us
    all_to_all x1, starting transfers between devices, local(): lax.all_to_all(height_back.reshape(TT * HH, band_count, chan_part), SP, s...  16.2 us
  transfers between devices with their start and end apart: 2, of which 1 were waited for; matrix products, arithmetic and copies ran while one was open for 2% of the time, Pallas kernels for 0%

commit v1 on v0

--- a/solution.py
+++ b/solution.py
@@ -33,7 +33,9 @@
 def gather_in_order(value, axes, sequence):
     parts = value[None]
     for k in sequence:
-        parts = lax.all_gather(parts, axes[k], axis=0, tiled=True)
+        parts = jnp.concatenate(
+            lax.all_to_all(jnp.stack([parts] * lax.axis_size(axes[k])), axes[k], 0, 0), axis=0
+        )
     held = [lax.axis_size(axes[k]) for k in reversed(sequence)]
     parts = parts.reshape(*held, *value.shape)
     turned = sorted(range(len(sequence)), key=lambda place: sequence[len(sequence) - 1 - place])

time: 583 us -> 569 us (0.976)
  blocking collectives: 238 us -> 14 us
  waiting for transfers between devices: 275 us -> 397 us
  starting transfers between devices: 16.2 us -> 102 us
    all_gather x2 -> x0, blocking collectives: 123 us -> none  [gather_in_order(): parts = lax.all_gather(parts, axes[k], axis=0, tiled=True)]
    all_to_all x1, waiting for transfers between devices: 0.01 us -> 101 us  [local(): lax.all_to_all(height_back.reshape(TT * HH, band_count, chan_part), SP, s...]
    all_to_all x1, blocking collectives: 104 us -> 6.24 us  [gather_in_order(): lax.all_to_all(jnp.stack([parts] * lax.axis_size(axes[k])), axes[k], 0, 0)]
    all_to_all x0 -> x3, starting transfers between devices: none -> 89.4 us  [the longest x2 69.9 us: gather_in_order(): lax.all_to_all(jnp.stack([parts] * lax.axis_size(axes[k])), axes[k], 0, 0)]
    all_to_all x0 -> x3, waiting for transfers between devices: none -> 84.2 us  [the longest x1 84.2 us: local(): lax.all_to_all(width_spec, SP, split_axis=1, concat_axis=0, tiled=True)]
    all_gather x1, waiting for transfers between devices: 275 us -> 211 us  [in_one_piece(): lax.all_gather(both, axis, axis=dim, tiled=True)]
    unnamed x1 -> x0, blocking collectives: 6.2 us -> none
  transfers between devices with their start and end apart: 2 -> 5, of which waited for: 1 -> 3; matrix products, arithmetic and copies ran while one was open for 2% -> 5% of each run, Pallas kernels for 0% -> 0%
where the time goes in v1:
time: 569 us; the launch traced here: 567 us
  waiting for transfers between devices  397 us (70%)
  starting transfers between devices  102 us (18%)
  local copies, waits for them, and re-layouts  20.4 us (4%)
  matrix products  15.8 us (3%)
  between operations  14.2 us (2%)
  blocking collectives  14 us (2%)
    all_gather x1, waiting for transfers between devices, in_one_piece(): lax.all_gather(both, axis, axis=dim, tiled=True)  211 us
    all_to_all x1, waiting for transfers between devices, local(): lax.all_to_all(height_back.reshape(TT * HH, band_count, chan_part), SP, s...  101 us
    all_to_all x1, waiting for transfers between devices, local(): lax.all_to_all(width_spec, SP, split_axis=1, concat_axis=0, tiled=True)  84.2 us
    all_to_all x2, starting transfers between devices, gather_in_order(): lax.all_to_all(jnp.stack([parts] * lax.axis_size(axes[k])), axes[k], 0, 0)  69.9 us
    all_to_all x1, starting transfers between devices, local(): lax.all_to_all(width_spec, SP, split_axis=1, concat_axis=0, tiled=True)  19.6 us
    all_to_all x1, starting transfers between devices, local(): lax.all_to_all(height_back.reshape(TT * HH, band_count, chan_part), SP, s...  12.4 us
  transfers between devices with their start and end apart: 5, of which 3 were waited for; matrix products, arithmetic and copies ran while one was open for 5% of the time, Pallas kernels for 0%

profile of v1, /device:TPU:39, one launch (start us, length us, event | category | flops | bytes accessed | tf_op | source)
XLA Modules:
  0.0 566.6 jit_solution(611881971577746218)
XLA Ops:
  6.5 0.0 all-gather.2.cloned.1.call-start
  6.6 1.3 pad_maximum_fusion
  7.9 0.1 all-gather.2.cloned.1.call-update
  8.0 0.0 copy-start
  8.0 0.0 copy-start.2
  8.0 6.7 %copy.52 = bf16[4,32768]{0,1:T(8,128)(2,1)} copy(bf16[4,32768]{1,0:T(4,128)(2,1)} %param.13) | data formatting | bytes 524288 | tf_op args[5]
  14.7 0.0 copy-done
  14.7 5.2 gather_fusion
  19.9 0.1 convert_reduce_fusion
  20.0 6.2 %all_to_all.67 = f32[4,1,4]{2,1,0:T(1,128)S(1)} all-to-all(f32[4,1,4]{2,1,0:T(1,128)S(1)} %stack.9), channel_id=1, replica_groups=mesh['grp'=2,'sp_0'=4,'sp_1'=32,'ch'=2] {'sp_0'}, dimensions={0} | all-to-all | bytes 128 | tf_op jit(solution)/shard_map/all_to_all | solution.py:37
  26.3 0.1 copy.53
  26.4 0.6 stack.10
  27.0 45.5 %all-to-all-start.3 = ((f32[32,4,4]{1,2,0:T(4,128)}), f32[32,4,4]{1,2,0:T(4,128)S(1)}, u32[]{:S(2)}, u32[]{:S(2)}) async-start(f32[32,4,4]{1,2,0:T(4,128)} %stack.10), calls=%async_computation.3 | async-start | bytes 131072 | tf_op jit(solution)/shard_map/all_to_all | solution.py:37
  72.5 211.1 %all-gather.2.cloned.1.call-done = bf16[1024,2048]{1,0:T(8,128)(2,1)} async-done(((bf16[8,2048]{1,0:T(8,128)(2,1)}), bf16[1024,2048]{1,0:T(8,128)(2,1)}) %all-gather.2.cloned.1.call-update) | async-done | bytes 4194320 | tf_op jit(solution)/shard_map/all_gather | solution.py:24
  283.6 0.0 copy-done.2
  283.6 2.5 fusion.11
  286.2 0.7 fusion.12
  286.9 1.7 copy.45
  288.6 0.0 all-to-all-done.3
  288.6 19.6 %all-to-all-start = ((bf16[8,128,512]{2,0,1:T(8,128)(2,1)}), bf16[8,128,512]{2,0,1:T(8,128)(2,1)S(1)}, u32[]{:S(2)}, u32[]{:S(2)}) async-start(bf16[8,128,512]{2,0,1:T(8,128)(2,1)} %copy.45), calls=%async_computation | async-start | bytes 2097152 | tf_op jit(solution)/shard_map/all_to_all | solution.py:82
  308.2 0.1 stack_reshape.5
  308.3 0.6 pad_maximum_fusion.1
  308.9 84.2 %all-to-all-done = bf16[8,128,512]{2,0,1:T(8,128)(2,1)S(1)} async-done(((bf16[8,128,512]{2,0,1:T(8,128)(2,1)}), bf16[8,128,512]{2,0,1:T(8,128)(2,1)S(1)}, u32[]{:S(2)}, u32[]{:S(2)}) %all-to-all-start) | async-done | bytes 1048608 | tf_op jit(solution)/shard_map/all_to_all | solution.py:82
  393.0 24.4 %all-to-all-start.4 = ((f32[2,128,4]{1,2,0:T(4,128)}), f32[2,128,4]{1,2,0:T(4,128)S(1)}, u32[]{:S(2)}, u32[]{:S(2)}) async-start(f32[2,128,4]{1,2,0:T(4,128)} %pad_maximum_fusion.1), calls=%async_computation.4 | async-start | bytes 8192 | tf_op jit(solution)/shard_map/all_to_all | solution.py:37
  417.4 0.5 fusion.14
  418.0 2.8 convolution_convert_fusion.2
  420.8 1.5 convolution_convert_fusion
  422.3 0.5 broadcast.88
  422.8 1.5 reduce.1
  424.3 1.2 reshape.70
  425.5 0.0 all-to-all-done.4
  425.5 12.4 %all-to-all-start.1 = ((bf16[128,2,2048]{2,1,0:T(2,128)(2,1)}), bf16[128,2,2048]{2,1,0:T(2,128)(2,1)S(1)}, u32[]{:S(2)}, u32[]{:S(2)}) async-start(bf16[128,2,2048]{2,1,0:T(2,128)(2,1)} %reshape.70), calls=%async_computation.1 | async-start | bytes 2097152 | tf_op jit(solution)/shard_map/all_to_all | solution.py:90
  438.5 0.1 reshape_reshape.6
  438.7 0.6 copy.55
  439.3 0.2 reshape_reshape.7
  439.5 0.1 fusion.76
  439.5 101.5 %all-to-all-done.1 = bf16[128,2,2048]{2,1,0:T(2,128)(2,1)S(1)} async-done(((bf16[128,2,2048]{2,1,0:T(2,128)(2,1)}), bf16[128,2,2048]{2,1,0:T(2,128)(2,1)S(1)}, u32[]{:S(2)}, u32[]{:S(2)}) %all-to-all-start.1) | async-done | bytes 1048608 | tf_op jit(solution)/shard_map/all_to_all | solution.py:90
  541.0 1.0 reshape.71
  542.1 0.3 copy.80
  542.4 1.1 fusion.20
  543.5 1.9 copy.51
  545.3 0.0 copy-start.3
  545.3 4.3 fusion.8
  549.7 0.0 copy-start.1
  549.7 0.1 copy.79
  549.7 7.7 %all_to_all.68 = bf16[2,512,512]{1,2,0:T(8,128)(2,1)S(1)} all-to-all(bf16[2,512,512]{1,2,0:T(8,128)(2,1)S(1)} %bitcast.99), channel_id=1, replica_groups=mesh['grp'=2,'sp_0'=4,'sp_1'=32,'ch'=2] {'ch'}, dimensions={0} | all-to-all | bytes 2097152 | tf_op jit(solution)/shard_map/all_to_all | solution.py:106
  557.5 0.0 copy-done.3
  557.5 0.0 copy-done.1
  557.5 2.3 add_convert_fusion
  (6 shorter events, 0.0 us)
Async XLA Ops:
  6.5 277.1 %all-gather.2.cloned.1.call-start = ((), (), s32[]{:S(2)}) async-start(), calls=%async_computation.6 | async-start | bytes 4227072 | tf_op jit(solution)/shard_map/all_gather | solution.py:24
  8.0 6.7 %copy-start = (s32[256]{0:T(256)S(1)}, s32[256]{0:T(256)}, u32[]{:S(2)}) copy-start(s32[256]{0:T(256)} %param.14) | copy-start | bytes 3076
  8.0 275.6 %copy-start.2 = (bf16[1024,1024]{1,0:T(8,128)(2,1)S(1)}, bf16[1024,1024]{1,0:T(8,128)(2,1)}, u32[]{:S(2)}) copy-start(bf16[1024,1024]{1,0:T(8,128)(2,1)} %param.8) | copy-start | bytes 6291460
  27.0 261.5 %all-to-all-start.3 = ((f32[32,4,4]{1,2,0:T(4,128)}), f32[32,4,4]{1,2,0:T(4,128)S(1)}, u32[]{:S(2)}, u32[]{:S(2)}) async-start(f32[32,4,4]{1,2,0:T(4,128)} %stack.10), calls=%async_computation.3 | async-start | bytes 131072 | tf_op jit(solution)/shard_map/all_to_all | solution.py:37
  288.6 104.5 %all-to-all-start = ((bf16[8,128,512]{2,0,1:T(8,128)(2,1)}), bf16[8,128,512]{2,0,1:T(8,128)(2,1)S(1)}, u32[]{:S(2)}, u32[]{:S(2)}) async-start(bf16[8,128,512]{2,0,1:T(8,128)(2,1)} %copy.45), calls=%async_computation | async-start | bytes 2097152 | tf_op jit(solution)/shard_map/all_to_all | solution.py:82
  393.0 32.5 %all-to-all-start.4 = ((f32[2,128,4]{1,2,0:T(4,128)}), f32[2,128,4]{1,2,0:T(4,128)S(1)}, u32[]{:S(2)}, u32[]{:S(2)}) async-start(f32[2,128,4]{1,2,0:T(4,128)} %pad_maximum_fusion.1), calls=%async_computation.4 | async-start | bytes 8192 | tf_op jit(solution)/shard_map/all_to_all | solution.py:37
  425.5 115.5 %all-to-all-start.1 = ((bf16[128,2,2048]{2,1,0:T(2,128)(2,1)}), bf16[128,2,2048]{2,1,0:T(2,128)(2,1)S(1)}, u32[]{:S(2)}, u32[]{:S(2)}) async-start(bf16[128,2,2048]{2,1,0:T(2,128)(2,1)} %reshape.70), calls=%async_computation.1 | async-start | bytes 2097152 | tf_op jit(solution)/shard_map/all_to_all | solution.py:90
  545.3 12.2 %copy-start.3 = (bf16[1024,1024]{1,0:T(8,128)(2,1)S(1)}, bf16[1024,1024]{1,0:T(8,128)(2,1)}, u32[]{:S(2)}) copy-start(bf16[1024,1024]{1,0:T(8,128)(2,1)} %param.8) | copy-start | bytes 6291460
  549.7 7.8 %copy-start.1 = (bf16[1024,2048]{1,0:T(8,128)(2,1)S(1)}, bf16[1024,2048]{1,0:T(8,128)(2,1)}, u32[]{:S(2)}) copy-start(bf16[1024,2048]{1,0:T(8,128)(2,1)} %all-gather.2.cloned.1.call-done) | copy-start | bytes 12582916
Sparse Core Ops, SparseCore 0:
  10.3 273.2 all-gather.1
